TPU v7x, 32 devices: a whole 2x2x4 slice. The times are simulated.
32 devices in a mesh: seed: 4 (over x, core), train: 8 (over z, y).
Axes of the slice: x: 2, y: 2, z: 4, core: 2. Of those that a mesh axis runs over, the one named last changes fastest.
Arguments:
- coordinates: float32 [16, 524288], P('seed', 'train'), parts along dimension 0, may hold values from -6 to 6
- slice_index: int32 [2097152], P(('seed', 'train')), parts along dimension 0, may hold values from 0 to 127, as said below
- history: float32 [32, 2, 128, 1024], P('seed', None, None, 'train'), parts along dimension 0, may hold values from -3 to 3
- impedance: float32 [9, 2, 1024], replicated, may hold values from -1.2 to 1.2
- slice_wake: float32 [128, 128], replicated, may hold values from -0.5 to 0.5
- tunes: float32 [8], P('seed'), parts along dimension 0, may hold values from 0.05 to 0.45
- detuning: float32 [8], P('seed'), parts along dimension 0, may hold values from 0.1 to 0.4
Outputs:
- tracked: float32 [16, 524288], P('seed', 'train'), parts along dimension 0
- moments: float32 [8, 128, 1024], P('seed', None, 'train'), parts along dimension 0
There are 4 independent parts, one for each index of `seed`. A program takes and returns all parts, laid end to end along the dimension named above; an argument that names none is the same for every part. Nothing has to cross between parts.
Inputs may be any that keep to these rules, and one draw needn't show every extreme that they name: `slice_index`: within each bunch, that is each aligned block of 512 entries, every slice number appears exactly 512 // 128 times.
All inputs are finite; a program needn't handle non-finite values.
Results may differ from a plain program's by a relative error of at most 0.00005.
Values sent between devices are 32-bit elements; how exact they have to be, the bound alone decides.
No kernel may reach another device: no remote copies, remote signals or barrier semaphores. Data moves between devices by JAX's collectives and lax.ppermute only.
A program may use at most 64 MiB of HBM per device.

v0:
```python
import math
import jax
import jax.numpy as jnp
from jax import lax
from jax.sharding import PartitionSpec as P

full_turn = 2.0 * math.pi


def rotate(positions, pushes, tunes, detuning):
    result = []
    for plane_index in range(2):
        position = positions[2 * plane_index]
        slope = positions[2 * plane_index + 1] + pushes[plane_index]
        action = 0.5 * (position * position + slope * slope)
        phase = full_turn * tunes[plane_index] + detuning[plane_index] * action
        cosine = jnp.cos(phase)
        sine = jnp.sin(phase)
        result.append(cosine * position + sine * slope)
        result.append(cosine * slope - sine * position)
    return jnp.stack(result)


def phase_tables(row_count, col_count, period):
    first = lax.broadcasted_iota(jnp.int32, (row_count, col_count), 0)
    second = lax.broadcasted_iota(jnp.int32, (row_count, col_count), 1)
    angle = full_turn / period * (first * second % period).astype(jnp.float32)
    return (jnp.cos(angle), jnp.sin(angle))


def contract(form, table, values):
    return jnp.einsum(form, table, values, precision=lax.Precision.HIGHEST)


def forward(series):
    item_count, column_count, bunch_total = series.shape
    trains = lax.axis_size("train")
    bunch_dev = bunch_total // trains
    signal = series.reshape(item_count, column_count, trains, bunch_dev)
    cos_train, sin_train = phase_tables(trains, trains, trains)
    first_re = contract("kp,ncpj->nckj", cos_train, signal)
    first_im = -contract("kp,ncpj->nckj", sin_train, signal)
    cos_twist, sin_twist = phase_tables(trains, bunch_dev, bunch_total)
    twist_re = first_re * cos_twist + first_im * sin_twist
    twist_im = first_im * cos_twist - first_re * sin_twist
    cos_local, sin_local = phase_tables(bunch_dev, bunch_dev, bunch_dev)
    spec_re = contract("qj,nckj->ncqk", cos_local, twist_re) + contract(
        "qj,nckj->ncqk", sin_local, twist_im
    )
    spec_im = contract("qj,nckj->ncqk", cos_local, twist_im) - contract(
        "qj,nckj->ncqk", sin_local, twist_re
    )
    return (
        spec_re.reshape(item_count, column_count, bunch_total),
        spec_im.reshape(item_count, column_count, bunch_total),
    )


def inverse(summed_re, summed_im):
    column_count, bunch_total = summed_re.shape
    trains = lax.axis_size("train")
    bunch_dev = bunch_total // trains
    grid_re = summed_re.reshape(column_count, bunch_dev, trains)
    grid_im = summed_im.reshape(column_count, bunch_dev, trains)
    cos_local, sin_local = phase_tables(bunch_dev, bunch_dev, bunch_dev)
    back_re = contract("qj,cqk->ckj", cos_local, grid_re) - contract(
        "qj,cqk->ckj", sin_local, grid_im
    )
    back_im = contract("qj,cqk->ckj", cos_local, grid_im) + contract(
        "qj,cqk->ckj", sin_local, grid_re
    )
    cos_twist, sin_twist = phase_tables(trains, bunch_dev, bunch_total)
    turned_re = back_re * cos_twist - back_im * sin_twist
    turned_im = back_re * sin_twist + back_im * cos_twist
    cos_train, sin_train = phase_tables(trains, trains, trains)
    field = (
        contract("kp,ckj->cpj", cos_train, turned_re)
        - contract("kp,ckj->cpj", sin_train, turned_im)
    ) / bunch_total
    return field.reshape(column_count, bunch_total)


def local(coordinates, slice_index, history, impedance, slice_wake, tunes, detuning):
    particle_count = slice_index.shape[0]
    slice_count = slice_wake.shape[0]
    bunch_dev = history.shape[3]
    turn_total = history.shape[0] + 1
    per_bunch = particle_count // bunch_dev
    bunch_group = math.gcd(bunch_dev, 16)
    group_count = bunch_dev // bunch_group
    group_span = bunch_group * per_bunch
    levels = lax.broadcasted_iota(jnp.int32, (1, 1, slice_count), 2)

    def selector(group_index):
        picked = lax.dynamic_slice_in_dim(slice_index, group_index * group_span, group_span)
        picked = picked.reshape(bunch_group, per_bunch)
        return (picked[:, :, None] == levels).astype(jnp.float32)

    def deposit(group_index, gathered):
        onehot = selector(group_index)
        section = lax.dynamic_slice_in_dim(coordinates, group_index * group_span, group_span, 1)
        transverse = section[0::2].reshape(2, bunch_group, per_bunch)
        sums = contract("gps,cgp->csg", onehot, transverse)
        return lax.dynamic_update_slice_in_dim(
            gathered, sums * (slice_count / per_bunch), group_index * bunch_group, 2
        )

    moments = lax.fori_loop(
        0, group_count, deposit, jnp.zeros((2, slice_count, bunch_dev), jnp.float32)
    )
    series = jnp.concatenate([moments[None], history], 0).reshape(
        turn_total, 2 * slice_count, bunch_dev
    )
    imp_re = impedance[:, 0, :]
    imp_im = impedance[:, 1, :]
    spec_re, spec_im = forward(
        lax.all_to_all(series, "train", split_axis=1, concat_axis=2, tiled=True)
    )
    summed_re = jnp.sum(imp_re[:, None, :] * spec_re - imp_im[:, None, :] * spec_im, axis=0)
    summed_im = jnp.sum(imp_re[:, None, :] * spec_im + imp_im[:, None, :] * spec_re, axis=0)
    field = inverse(summed_re, summed_im)
    home = lax.all_to_all(field, "train", split_axis=1, concat_axis=0, tiled=True).reshape(
        2, slice_count, bunch_dev
    )
    kicks = contract("st,ctb->csb", slice_wake, home)

    def track(group_index, moved):
        onehot = selector(group_index)
        local_kicks = lax.dynamic_slice_in_dim(kicks, group_index * bunch_group, bunch_group, 2)
        pushes = contract("gps,csg->cgp", onehot, local_kicks).reshape(2, group_span)
        section = lax.dynamic_slice_in_dim(coordinates, group_index * group_span, group_span, 1)
        turned = rotate(section, pushes, tunes, detuning)
        return lax.dynamic_update_slice_in_dim(moved, turned, group_index * group_span, 1)

    tracked = lax.fori_loop(0, group_count, track, jnp.zeros_like(coordinates))
    return (tracked, moments)


def solution(mesh):
    return jax.shard_map(
        local,
        mesh=mesh,
        in_specs=(
            P("seed", "train"),
            P(("seed", "train")),
            P("seed", None, None, "train"),
            P(),
            P(),
            P("seed"),
            P("seed"),
        ),
        out_specs=(P("seed", "train"), P("seed", None, "train")),
        check_vma=False,
    )
```

profile of v0, /device:TPU:0, one launch (start us, length us, event | category | flops | bytes accessed | tf_op | source)
XLA Modules:
  0.0 208.2 jit_solution(1865617908062196139)
XLA Ops:
  0.7 37.9 %while.30 = (s32[]{:T(128)}, f32[2,128,128]{1,0,2:T(2,128)S(1)}, f32[4,65536]{1,0:T(4,128)}, s32[65536]{0:T(1024)}, s32[]{:T(128)}, /*index=5*/s32[]{:T(128)}, s32[]{:T(128)}, s32[]{:T(128)}, s32[]{:T(128)}, s32[]{:T(128)}) while((s32[]{:T(128)}, f32[2,128,128]{1,0,2:T(2,128)S(1)}, f32[4,65536]{1,0:T(4,128)}, s32[65536]{0:T(1024)}, ...), condition=%wide.region_1.0_spmd.clone, body=%wide.region_0.0_spmd.clone.sunk | while | flops 26218504 | bytes 639181 | solution.py:108
  3.1 2.4 %fusion.152 = f32[2,128,128]{1,0,2:T(2,128)S(1)} fusion(f32[2,128,128]{1,0,2:T(2,128)S(1)} %get-tuple-element.530, s32[]{:T(128)S(6)} %select_n.184, f32[2,16,512]{2,0,1:T(2,128)S(1)} %bitcast.100, s32[16,512]{1,0:T(8,128)S(1)} %eq.147), kind=kOutput, calls=%fused_computation.7.clone.1 | convolution fusion | flops 26218496 | bytes 114692 | tf_op jit(solution)/shard_map/while/body/eval_jaxpr/gps,cgp->csg/dot_general | solution.py:32
  7.8 2.4 %fusion.152 = f32[2,128,128]{1,0,2:T(2,128)S(1)} fusion(f32[2,128,128]{1,0,2:T(2,128)S(1)} %get-tuple-element.530, s32[]{:T(128)S(6)} %select_n.184, f32[2,16,512]{2,0,1:T(2,128)S(1)} %bitcast.100, s32[16,512]{1,0:T(8,128)S(1)} %eq.147), kind=kOutput, calls=%fused_computation.7.clone.1 | convolution fusion | flops 26218496 | bytes 114692 | tf_op jit(solution)/shard_map/while/body/eval_jaxpr/gps,cgp->csg/dot_general | solution.py:32
  12.5 2.4 %fusion.152 = f32[2,128,128]{1,0,2:T(2,128)S(1)} fusion(f32[2,128,128]{1,0,2:T(2,128)S(1)} %get-tuple-element.530, s32[]{:T(128)S(6)} %select_n.184, f32[2,16,512]{2,0,1:T(2,128)S(1)} %bitcast.100, s32[16,512]{1,0:T(8,128)S(1)} %eq.147), kind=kOutput, calls=%fused_computation.7.clone.1 | convolution fusion | flops 26218496 | bytes 114692 | tf_op jit(solution)/shard_map/while/body/eval_jaxpr/gps,cgp->csg/dot_general | solution.py:32
  17.3 2.4 %fusion.152 = f32[2,128,128]{1,0,2:T(2,128)S(1)} fusion(f32[2,128,128]{1,0,2:T(2,128)S(1)} %get-tuple-element.530, s32[]{:T(128)S(6)} %select_n.184, f32[2,16,512]{2,0,1:T(2,128)S(1)} %bitcast.100, s32[16,512]{1,0:T(8,128)S(1)} %eq.147), kind=kOutput, calls=%fused_computation.7.clone.1 | convolution fusion | flops 26218496 | bytes 114692 | tf_op jit(solution)/shard_map/while/body/eval_jaxpr/gps,cgp->csg/dot_general | solution.py:32
  22.0 2.4 %fusion.152 = f32[2,128,128]{1,0,2:T(2,128)S(1)} fusion(f32[2,128,128]{1,0,2:T(2,128)S(1)} %get-tuple-element.530, s32[]{:T(128)S(6)} %select_n.184, f32[2,16,512]{2,0,1:T(2,128)S(1)} %bitcast.100, s32[16,512]{1,0:T(8,128)S(1)} %eq.147), kind=kOutput, calls=%fused_computation.7.clone.1 | convolution fusion | flops 26218496 | bytes 114692 | tf_op jit(solution)/shard_map/while/body/eval_jaxpr/gps,cgp->csg/dot_general | solution.py:32
  26.7 2.4 %fusion.152 = f32[2,128,128]{1,0,2:T(2,128)S(1)} fusion(f32[2,128,128]{1,0,2:T(2,128)S(1)} %get-tuple-element.530, s32[]{:T(128)S(6)} %select_n.184, f32[2,16,512]{2,0,1:T(2,128)S(1)} %bitcast.100, s32[16,512]{1,0:T(8,128)S(1)} %eq.147), kind=kOutput, calls=%fused_computation.7.clone.1 | convolution fusion | flops 26218496 | bytes 114692 | tf_op jit(solution)/shard_map/while/body/eval_jaxpr/gps,cgp->csg/dot_general | solution.py:32
  31.5 2.4 %fusion.152 = f32[2,128,128]{1,0,2:T(2,128)S(1)} fusion(f32[2,128,128]{1,0,2:T(2,128)S(1)} %get-tuple-element.530, s32[]{:T(128)S(6)} %select_n.184, f32[2,16,512]{2,0,1:T(2,128)S(1)} %bitcast.100, s32[16,512]{1,0:T(8,128)S(1)} %eq.147), kind=kOutput, calls=%fused_computation.7.clone.1 | convolution fusion | flops 26218496 | bytes 114692 | tf_op jit(solution)/shard_map/while/body/eval_jaxpr/gps,cgp->csg/dot_general | solution.py:32
  36.2 2.4 %fusion.152 = f32[2,128,128]{1,0,2:T(2,128)S(1)} fusion(f32[2,128,128]{1,0,2:T(2,128)S(1)} %get-tuple-element.530, s32[]{:T(128)S(6)} %select_n.184, f32[2,16,512]{2,0,1:T(2,128)S(1)} %bitcast.100, s32[16,512]{1,0:T(8,128)S(1)} %eq.147), kind=kOutput, calls=%fused_computation.7.clone.1 | convolution fusion | flops 26218496 | bytes 114692 | tf_op jit(solution)/shard_map/while/body/eval_jaxpr/gps,cgp->csg/dot_general | solution.py:32
  41.0 7.4 %all-to-all-start = ((f32[9,256,128]{2,0,1:T(8,128)}), f32[9,256,128]{2,0,1:T(8,128)S(1)}, u32[]{:S(2)}, u32[]{:S(2)}) async-start(f32[9,256,128]{2,0,1:T(8,128)} %pad_maximum_fusion), calls=%async_computation | async-start | bytes 4194304 | tf_op jit(solution)/shard_map/all_to_all | solution.py:117
  49.8 46.9 %all-to-all-done = f32[9,256,128]{2,0,1:T(8,128)S(1)} async-done(((f32[9,256,128]{2,0,1:T(8,128)}), f32[9,256,128]{2,0,1:T(8,128)S(1)}, u32[]{:S(2)}, u32[]{:S(2)}) %all-to-all-start) | async-done | bytes 1179680 | tf_op jit(solution)/shard_map/all_to_all | solution.py:117
  109.7 3.6 %all-to-all-start.1 = ((f32[32,8,128]{2,0,1:T(8,128)}), f32[32,8,128]{2,0,1:T(8,128)S(1)}, u32[]{:S(2)}, u32[]{:S(2)}) async-start(f32[32,8,128]{2,0,1:T(8,128)} %copy.34), calls=%async_computation.1 | async-start | bytes 262144 | tf_op jit(solution)/shard_map/all_to_all | solution.py:122
  117.0 3.7 %all-to-all-done.1 = f32[32,8,128]{2,0,1:T(8,128)S(1)} async-done(((f32[32,8,128]{2,0,1:T(8,128)}), f32[32,8,128]{2,0,1:T(8,128)S(1)}, u32[]{:S(2)}, u32[]{:S(2)}) %all-to-all-start.1) | async-done | bytes 131104 | tf_op jit(solution)/shard_map/all_to_all | solution.py:122
  121.2 86.0 %while.31 = (s32[]{:T(128)}, f32[4,65536]{1,0:T(4,128)S(1)}, f32[]{:T(128)}, f32[4,65536]{1,0:T(4,128)}, f32[2,128,128]{1,2,0:T(8,128)S(1)}, /*index=5*/s32[6553...) while((s32[]{:T(128)}, f32[4,65536]{1,0:T(4,128)S(1)}, ...), condition=%wide.region_5.6_spmd.clone, body=%wide.region_4.5_spmd.clone.sunk | while | flops 26509320 | bytes 1458525 | solution.py:135
  122.0 2.9 %fusion.154 = f32[2,16,512]{2,0,1:T(2,128)S(1)} fusion(s32[16,512]{1,0:T(8,128)S(1)} %eq.150, f32[2,128,16]{1,2,0:T(8,128)S(1)} %constant_dynamic-slice_fusion.5), kind=kOutput, calls=%fused_computation.12.clone.1 | convolution fusion | flops 26214400 | bytes 114688 | tf_op jit(solution)/shard_map/while/body/eval_jaxpr/gps,csg->cgp/dot_general | solution.py:32
  127.0 3.0 %multiply_add_fusion.11 = (f32[1,8192]{1,0:T(1,128)S(1)}, f32[1,8192]{1,0:T(1,128)S(1)}, f32[1,8192]{1,0:T(1,128)S(1)}, f32[1,8192]{1,0:T(1,128)S(1)}, f32[1,8192]{1,0:T(1,128)S(1)}) fusion(f32[1,8192]{1,0:T(1,128)S(1)} %get-tuple-element.508, f32[1,8192]{1,0:T(1,128)S(1)} %get-tuple-element.509, f32[4,65536]{1,0:T(4,128)} %get-tuple-element.588, ...), kind=kLoop, calls=%fused_computation.20.clone.1 | loop fusion | flops 98304 | bytes 393236 | tf_op jit(solution)/shard_map/while/body/eval_jaxpr/add | solution.py:19
  132.8 2.9 %fusion.154 = f32[2,16,512]{2,0,1:T(2,128)S(1)} fusion(s32[16,512]{1,0:T(8,128)S(1)} %eq.150, f32[2,128,16]{1,2,0:T(8,128)S(1)} %constant_dynamic-slice_fusion.5), kind=kOutput, calls=%fused_computation.12.clone.1 | convolution fusion | flops 26214400 | bytes 114688 | tf_op jit(solution)/shard_map/while/body/eval_jaxpr/gps,csg->cgp/dot_general | solution.py:32
  135.8 1.9 fusion.156
  137.7 3.0 %multiply_add_fusion.11 = (f32[1,8192]{1,0:T(1,128)S(1)}, f32[1,8192]{1,0:T(1,128)S(1)}, f32[1,8192]{1,0:T(1,128)S(1)}, f32[1,8192]{1,0:T(1,128)S(1)}, f32[1,8192]{1,0:T(1,128)S(1)}) fusion(f32[1,8192]{1,0:T(1,128)S(1)} %get-tuple-element.508, f32[1,8192]{1,0:T(1,128)S(1)} %get-tuple-element.509, f32[4,65536]{1,0:T(4,128)} %get-tuple-element.588, ...), kind=kLoop, calls=%fused_computation.20.clone.1 | loop fusion | flops 98304 | bytes 393236 | tf_op jit(solution)/shard_map/while/body/eval_jaxpr/add | solution.py:19
  143.5 2.9 %fusion.154 = f32[2,16,512]{2,0,1:T(2,128)S(1)} fusion(s32[16,512]{1,0:T(8,128)S(1)} %eq.150, f32[2,128,16]{1,2,0:T(8,128)S(1)} %constant_dynamic-slice_fusion.5), kind=kOutput, calls=%fused_computation.12.clone.1 | convolution fusion | flops 26214400 | bytes 114688 | tf_op jit(solution)/shard_map/while/body/eval_jaxpr/gps,csg->cgp/dot_general | solution.py:32
  146.5 1.9 fusion.156
  148.5 3.0 %multiply_add_fusion.11 = (f32[1,8192]{1,0:T(1,128)S(1)}, f32[1,8192]{1,0:T(1,128)S(1)}, f32[1,8192]{1,0:T(1,128)S(1)}, f32[1,8192]{1,0:T(1,128)S(1)}, f32[1,8192]{1,0:T(1,128)S(1)}) fusion(f32[1,8192]{1,0:T(1,128)S(1)} %get-tuple-element.508, f32[1,8192]{1,0:T(1,128)S(1)} %get-tuple-element.509, f32[4,65536]{1,0:T(4,128)} %get-tuple-element.588, ...), kind=kLoop, calls=%fused_computation.20.clone.1 | loop fusion | flops 98304 | bytes 393236 | tf_op jit(solution)/shard_map/while/body/eval_jaxpr/add | solution.py:19
  154.3 2.9 %fusion.154 = f32[2,16,512]{2,0,1:T(2,128)S(1)} fusion(s32[16,512]{1,0:T(8,128)S(1)} %eq.150, f32[2,128,16]{1,2,0:T(8,128)S(1)} %constant_dynamic-slice_fusion.5), kind=kOutput, calls=%fused_computation.12.clone.1 | convolution fusion | flops 26214400 | bytes 114688 | tf_op jit(solution)/shard_map/while/body/eval_jaxpr/gps,csg->cgp/dot_general | solution.py:32
  159.2 3.0 %multiply_add_fusion.11 = (f32[1,8192]{1,0:T(1,128)S(1)}, f32[1,8192]{1,0:T(1,128)S(1)}, f32[1,8192]{1,0:T(1,128)S(1)}, f32[1,8192]{1,0:T(1,128)S(1)}, f32[1,8192]{1,0:T(1,128)S(1)}) fusion(f32[1,8192]{1,0:T(1,128)S(1)} %get-tuple-element.508, f32[1,8192]{1,0:T(1,128)S(1)} %get-tuple-element.509, f32[4,65536]{1,0:T(4,128)} %get-tuple-element.588, ...), kind=kLoop, calls=%fused_computation.20.clone.1 | loop fusion | flops 98304 | bytes 393236 | tf_op jit(solution)/shard_map/while/body/eval_jaxpr/add | solution.py:19
  165.0 2.9 %fusion.154 = f32[2,16,512]{2,0,1:T(2,128)S(1)} fusion(s32[16,512]{1,0:T(8,128)S(1)} %eq.150, f32[2,128,16]{1,2,0:T(8,128)S(1)} %constant_dynamic-slice_fusion.5), kind=kOutput, calls=%fused_computation.12.clone.1 | convolution fusion | flops 26214400 | bytes 114688 | tf_op jit(solution)/shard_map/while/body/eval_jaxpr/gps,csg->cgp/dot_general | solution.py:32
  170.0 3.0 %multiply_add_fusion.11 = (f32[1,8192]{1,0:T(1,128)S(1)}, f32[1,8192]{1,0:T(1,128)S(1)}, f32[1,8192]{1,0:T(1,128)S(1)}, f32[1,8192]{1,0:T(1,128)S(1)}, f32[1,8192]{1,0:T(1,128)S(1)}) fusion(f32[1,8192]{1,0:T(1,128)S(1)} %get-tuple-element.508, f32[1,8192]{1,0:T(1,128)S(1)} %get-tuple-element.509, f32[4,65536]{1,0:T(4,128)} %get-tuple-element.588, ...), kind=kLoop, calls=%fused_computation.20.clone.1 | loop fusion | flops 98304 | bytes 393236 | tf_op jit(solution)/shard_map/while/body/eval_jaxpr/add | solution.py:19
  175.8 2.9 %fusion.154 = f32[2,16,512]{2,0,1:T(2,128)S(1)} fusion(s32[16,512]{1,0:T(8,128)S(1)} %eq.150, f32[2,128,16]{1,2,0:T(8,128)S(1)} %constant_dynamic-slice_fusion.5), kind=kOutput, calls=%fused_computation.12.clone.1 | convolution fusion | flops 26214400 | bytes 114688 | tf_op jit(solution)/shard_map/while/body/eval_jaxpr/gps,csg->cgp/dot_general | solution.py:32
  180.7 3.0 %multiply_add_fusion.11 = (f32[1,8192]{1,0:T(1,128)S(1)}, f32[1,8192]{1,0:T(1,128)S(1)}, f32[1,8192]{1,0:T(1,128)S(1)}, f32[1,8192]{1,0:T(1,128)S(1)}, f32[1,8192]{1,0:T(1,128)S(1)}) fusion(f32[1,8192]{1,0:T(1,128)S(1)} %get-tuple-element.508, f32[1,8192]{1,0:T(1,128)S(1)} %get-tuple-element.509, f32[4,65536]{1,0:T(4,128)} %get-tuple-element.588, ...), kind=kLoop, calls=%fused_computation.20.clone.1 | loop fusion | flops 98304 | bytes 393236 | tf_op jit(solution)/shard_map/while/body/eval_jaxpr/add | solution.py:19
  186.5 2.9 %fusion.154 = f32[2,16,512]{2,0,1:T(2,128)S(1)} fusion(s32[16,512]{1,0:T(8,128)S(1)} %eq.150, f32[2,128,16]{1,2,0:T(8,128)S(1)} %constant_dynamic-slice_fusion.5), kind=kOutput, calls=%fused_computation.12.clone.1 | convolution fusion | flops 26214400 | bytes 114688 | tf_op jit(solution)/shard_map/while/body/eval_jaxpr/gps,csg->cgp/dot_general | solution.py:32
  191.5 3.0 %multiply_add_fusion.11 = (f32[1,8192]{1,0:T(1,128)S(1)}, f32[1,8192]{1,0:T(1,128)S(1)}, f32[1,8192]{1,0:T(1,128)S(1)}, f32[1,8192]{1,0:T(1,128)S(1)}, f32[1,8192]{1,0:T(1,128)S(1)}) fusion(f32[1,8192]{1,0:T(1,128)S(1)} %get-tuple-element.508, f32[1,8192]{1,0:T(1,128)S(1)} %get-tuple-element.509, f32[4,65536]{1,0:T(4,128)} %get-tuple-element.588, ...), kind=kLoop, calls=%fused_computation.20.clone.1 | loop fusion | flops 98304 | bytes 393236 | tf_op jit(solution)/shard_map/while/body/eval_jaxpr/add | solution.py:19
  197.3 2.9 %fusion.154 = f32[2,16,512]{2,0,1:T(2,128)S(1)} fusion(s32[16,512]{1,0:T(8,128)S(1)} %eq.150, f32[2,128,16]{1,2,0:T(8,128)S(1)} %constant_dynamic-slice_fusion.5), kind=kOutput, calls=%fused_computation.12.clone.1 | convolution fusion | flops 26214400 | bytes 114688 | tf_op jit(solution)/shard_map/while/body/eval_jaxpr/gps,csg->cgp/dot_general | solution.py:32
  202.2 3.0 %multiply_add_fusion.11 = (f32[1,8192]{1,0:T(1,128)S(1)}, f32[1,8192]{1,0:T(1,128)S(1)}, f32[1,8192]{1,0:T(1,128)S(1)}, f32[1,8192]{1,0:T(1,128)S(1)}, f32[1,8192]{1,0:T(1,128)S(1)}) fusion(f32[1,8192]{1,0:T(1,128)S(1)} %get-tuple-element.508, f32[1,8192]{1,0:T(1,128)S(1)} %get-tuple-element.509, f32[4,65536]{1,0:T(4,128)} %get-tuple-element.588, ...), kind=kLoop, calls=%fused_computation.20.clone.1 | loop fusion | flops 98304 | bytes 393236 | tf_op jit(solution)/shard_map/while/body/eval_jaxpr/add | solution.py:19
  (127 shorter events, 71.9 us)
Async XLA Ops:
  0.6 120.0 %copy-start = (f32[128,128]{1,0:T(8,128)S(1)}, f32[128,128]{1,0:T(8,128)}, u32[]{:S(2)}) copy-start(f32[128,128]{1,0:T(8,128)} %param.15) | copy-start | bytes 196612
  0.7 38.1 %copy-start.1 = (f32[8,2,128,128]{3,2,1,0:T(8,128)S(1)}, f32[8,2,128,128]{3,2,1,0:T(8,128)}, u32[]{:S(2)}) copy-start(f32[8,2,128,128]{3,2,1,0:T(8,128)} %param.13) | copy-start | bytes 3145732
  38.8 2.2 %copy-start.3 = (f32[2,128,128]{2,1,0:T(8,128)}, f32[2,128,128]{2,1,0:T(8,128)S(1)}, u32[]{:S(2)}) copy-start(f32[2,128,128]{2,1,0:T(8,128)S(1)} %copy.27) | copy-start | bytes 393220
  41.0 7.4 %copy-start.4 = (f32[9,2,1024]{2,1,0:T(2,128)S(1)}, f32[9,2,1024]{2,1,0:T(2,128)}, u32[]{:S(2)}) copy-start(f32[9,2,1024]{2,1,0:T(2,128)} %param.14) | copy-start | bytes 221188
  41.0 55.7 %all-to-all-start = ((f32[9,256,128]{2,0,1:T(8,128)}), f32[9,256,128]{2,0,1:T(8,128)S(1)}, u32[]{:S(2)}, u32[]{:S(2)}) async-start(f32[9,256,128]{2,0,1:T(8,128)} %pad_maximum_fusion), calls=%async_computation | async-start | bytes 4194304 | tf_op jit(solution)/shard_map/all_to_all | solution.py:117
  107.1 6.2 %copy-start.5 = (f32[2]{0:T(128)S(1)}, f32[2]{0:T(128)}, u32[]{:S(2)}) copy-start(f32[2]{0:T(128)} %param.16) | copy-start | bytes 28
  107.2 8.0 %copy-start.6 = (f32[2]{0:T(128)S(1)}, f32[2]{0:T(128)}, u32[]{:S(2)}) copy-start(f32[2]{0:T(128)} %param.17) | copy-start | bytes 28
  109.7 11.0 %all-to-all-start.1 = ((f32[32,8,128]{2,0,1:T(8,128)}), f32[32,8,128]{2,0,1:T(8,128)S(1)}, u32[]{:S(2)}, u32[]{:S(2)}) async-start(f32[32,8,128]{2,0,1:T(8,128)} %copy.34), calls=%async_computation.1 | async-start | bytes 262144 | tf_op jit(solution)/shard_map/all_to_all | solution.py:122
  207.2 1.0 copy-start.2
where the time goes:
time: 210 us; the launch traced here: 208 us
  other arithmetic  57 us (27%)
  matrix products  55.4 us (26%)
  waiting for transfers between devices  50.5 us (24%)
  local copies, waits for them, and re-layouts  30 us (14%)
  starting transfers between devices  11.1 us (5%)
  between operations  3.32 us (2%)
    dot_general x29, matrix products, contract(): return jnp.einsum(form, table, values, precision=lax.Precision.HIGHEST)  55.4 us
    all_to_all x1, waiting for transfers between devices, local(): lax.all_to_all(series, 'train', split_axis=1, concat_axis=2, tiled=True)  46.9 us
    add x16, other arithmetic, rotate(): result.append(cosine * position + sine * slope)  38.6 us
    cos x8, other arithmetic, rotate(): cosine = jnp.cos(phase)  15.5 us
    dynamic_slice x16, local copies, waits for them, and re-layouts, selector(): lax.dynamic_slice_in_dim(slice_index, group_index * group_span, group_span)  12.3 us
    all_to_all x1, starting transfers between devices, local(): lax.all_to_all(series, 'train', split_axis=1, concat_axis=2, tiled=True)  7.44 us
    dynamic_slice x8, local copies, waits for them, and re-layouts, deposit(): lax.dynamic_slice_in_dim(coordinates, group_index * group_span, group_spa...  7.43 us
    slice x8, local copies, waits for them, and re-layouts, deposit(): transverse = section[0::2].reshape(2, bunch_group, per_bunch)  4.52 us
  transfers between devices with their start and end apart: 2, of which 2 were waited for; matrix products, arithmetic and copies ran while one was open for 1% of the time, Pallas kernels for 0%

commit v1 on v0

--- a/solution.py
+++ b/solution.py
@@ -5,6 +5,12 @@
 from jax.sharding import PartitionSpec as P
 
 full_turn = 2.0 * math.pi
+
+
+def swap_blocks(block, axis, split, join):
+    cells = jnp.split(block, lax.axis_size(axis), axis=split)
+    received = lax.all_to_all(jnp.stack(cells), axis, 0, 0)
+    return jnp.concatenate(received, axis=join)
 
 
 def rotate(positions, pushes, tunes, detuning):
@@ -113,9 +119,7 @@
     )
     imp_re = impedance[:, 0, :]
     imp_im = impedance[:, 1, :]
-    spec_re, spec_im = forward(
-        lax.all_to_all(series, "train", split_axis=1, concat_axis=2, tiled=True)
-    )
+    spec_re, spec_im = forward(swap_blocks(series, "train", 1, 2))
     summed_re = jnp.sum(imp_re[:, None, :] * spec_re - imp_im[:, None, :] * spec_im, axis=0)
     summed_im = jnp.sum(imp_re[:, None, :] * spec_im + imp_im[:, None, :] * spec_re, axis=0)
     field = inverse(summed_re, summed_im)

time: 210 us -> 194 us (0.924)
  waiting for transfers between devices: 50.5 us -> 30.9 us
  other arithmetic: 57 us -> 60.8 us
    all_to_all x1, waiting for transfers between devices: 46.9 us -> 27.2 us  [swap_blocks(): received = lax.all_to_all(jnp.stack(cells), axis, 0, 0)]
    unnamed x0 -> x7, other arithmetic: none -> 4.68 us
where the time goes in v1:
time: 194 us; the launch traced here: 192 us
  other arithmetic  60.8 us (31%)
  matrix products  55.4 us (29%)
  waiting for transfers between devices  30.9 us (16%)
  local copies, waits for them, and re-layouts  29.3 us (15%)
  starting transfers between devices  11.1 us (6%)
  between operations  3.32 us (2%)
    dot_general x29, matrix products, contract(): return jnp.einsum(form, table, values, precision=lax.Precision.HIGHEST)  55.4 us
    add x16, other arithmetic, rotate(): result.append(cosine * position + sine * slope)  38.6 us
    all_to_all x1, waiting for transfers between devices, swap_blocks(): received = lax.all_to_all(jnp.stack(cells), axis, 0, 0)  27.2 us
    cos x8, other arithmetic, rotate(): cosine = jnp.cos(phase)  15.5 us
    dynamic_slice x16, local copies, waits for them, and re-layouts, selector(): lax.dynamic_slice_in_dim(slice_index, group_index * group_span, group_span)  12.3 us
    all_to_all x1, starting transfers between devices, swap_blocks(): received = lax.all_to_all(jnp.stack(cells), axis, 0, 0)  7.44 us
    dynamic_slice x8, local copies, waits for them, and re-layouts, deposit(): lax.dynamic_slice_in_dim(coordinates, group_index * group_span, group_spa...  7.43 us
    unnamed x7, other arithmetic  4.68 us
  transfers between devices with their start and end apart: 2, of which 2 were waited for; matrix products, arithmetic and copies ran while one was open for 1% of the time, Pallas kernels for 0%

profile of v1, /device:TPU:0, one launch (start us, length us, event | category | flops | bytes accessed | tf_op | source)
XLA Modules:
  0.0 191.6 jit_solution(5758421950268604145)
XLA Ops:
  0.7 37.9 %while.30 = (s32[]{:T(128)}, f32[2,128,128]{1,0,2:T(2,128)S(1)}, f32[4,65536]{1,0:T(4,128)}, s32[65536]{0:T(1024)}, s32[]{:T(128)}, /*index=5*/s32[]{:T(128)}, s32[]{:T(128)}, s32[]{:T(128)}, s32[]{:T(128)}, s32[]{:T(128)}) while((s32[]{:T(128)}, f32[2,128,128]{1,0,2:T(2,128)S(1)}, f32[4,65536]{1,0:T(4,128)}, s32[65536]{0:T(1024)}, ...), condition=%wide.region_1.0_spmd.clone, body=%wide.region_0.0_spmd.clone.sunk | while | flops 26218504 | bytes 639181 | solution.py:114
  3.1 2.4 %fusion.175 = f32[2,128,128]{1,0,2:T(2,128)S(1)} fusion(f32[2,128,128]{1,0,2:T(2,128)S(1)} %get-tuple-element.530, s32[]{:T(128)S(6)} %select_n.184, f32[2,16,512]{2,0,1:T(2,128)S(1)} %bitcast.144, s32[16,512]{1,0:T(8,128)S(1)} %eq.147), kind=kOutput, calls=%fused_computation.7.clone.1 | convolution fusion | flops 26218496 | bytes 114692 | tf_op jit(solution)/shard_map/while/body/eval_jaxpr/gps,cgp->csg/dot_general | solution.py:38
  7.8 2.4 %fusion.175 = f32[2,128,128]{1,0,2:T(2,128)S(1)} fusion(f32[2,128,128]{1,0,2:T(2,128)S(1)} %get-tuple-element.530, s32[]{:T(128)S(6)} %select_n.184, f32[2,16,512]{2,0,1:T(2,128)S(1)} %bitcast.144, s32[16,512]{1,0:T(8,128)S(1)} %eq.147), kind=kOutput, calls=%fused_computation.7.clone.1 | convolution fusion | flops 26218496 | bytes 114692 | tf_op jit(solution)/shard_map/while/body/eval_jaxpr/gps,cgp->csg/dot_general | solution.py:38
  12.5 2.4 %fusion.175 = f32[2,128,128]{1,0,2:T(2,128)S(1)} fusion(f32[2,128,128]{1,0,2:T(2,128)S(1)} %get-tuple-element.530, s32[]{:T(128)S(6)} %select_n.184, f32[2,16,512]{2,0,1:T(2,128)S(1)} %bitcast.144, s32[16,512]{1,0:T(8,128)S(1)} %eq.147), kind=kOutput, calls=%fused_computation.7.clone.1 | convolution fusion | flops 26218496 | bytes 114692 | tf_op jit(solution)/shard_map/while/body/eval_jaxpr/gps,cgp->csg/dot_general | solution.py:38
  17.3 2.4 %fusion.175 = f32[2,128,128]{1,0,2:T(2,128)S(1)} fusion(f32[2,128,128]{1,0,2:T(2,128)S(1)} %get-tuple-element.530, s32[]{:T(128)S(6)} %select_n.184, f32[2,16,512]{2,0,1:T(2,128)S(1)} %bitcast.144, s32[16,512]{1,0:T(8,128)S(1)} %eq.147), kind=kOutput, calls=%fused_computation.7.clone.1 | convolution fusion | flops 26218496 | bytes 114692 | tf_op jit(solution)/shard_map/while/body/eval_jaxpr/gps,cgp->csg/dot_general | solution.py:38
  22.0 2.4 %fusion.175 = f32[2,128,128]{1,0,2:T(2,128)S(1)} fusion(f32[2,128,128]{1,0,2:T(2,128)S(1)} %get-tuple-element.530, s32[]{:T(128)S(6)} %select_n.184, f32[2,16,512]{2,0,1:T(2,128)S(1)} %bitcast.144, s32[16,512]{1,0:T(8,128)S(1)} %eq.147), kind=kOutput, calls=%fused_computation.7.clone.1 | convolution fusion | flops 26218496 | bytes 114692 | tf_op jit(solution)/shard_map/while/body/eval_jaxpr/gps,cgp->csg/dot_general | solution.py:38
  26.7 2.4 %fusion.175 = f32[2,128,128]{1,0,2:T(2,128)S(1)} fusion(f32[2,128,128]{1,0,2:T(2,128)S(1)} %get-tuple-element.530, s32[]{:T(128)S(6)} %select_n.184, f32[2,16,512]{2,0,1:T(2,128)S(1)} %bitcast.144, s32[16,512]{1,0:T(8,128)S(1)} %eq.147), kind=kOutput, calls=%fused_computation.7.clone.1 | convolution fusion | flops 26218496 | bytes 114692 | tf_op jit(solution)/shard_map/while/body/eval_jaxpr/gps,cgp->csg/dot_general | solution.py:38
  31.5 2.4 %fusion.175 = f32[2,128,128]{1,0,2:T(2,128)S(1)} fusion(f32[2,128,128]{1,0,2:T(2,128)S(1)} %get-tuple-element.530, s32[]{:T(128)S(6)} %select_n.184, f32[2,16,512]{2,0,1:T(2,128)S(1)} %bitcast.144, s32[16,512]{1,0:T(8,128)S(1)} %eq.147), kind=kOutput, calls=%fused_computation.7.clone.1 | convolution fusion | flops 26218496 | bytes 114692 | tf_op jit(solution)/shard_map/while/body/eval_jaxpr/gps,cgp->csg/dot_general | solution.py:38
  36.2 2.4 %fusion.175 = f32[2,128,128]{1,0,2:T(2,128)S(1)} fusion(f32[2,128,128]{1,0,2:T(2,128)S(1)} %get-tuple-element.530, s32[]{:T(128)S(6)} %select_n.184, f32[2,16,512]{2,0,1:T(2,128)S(1)} %bitcast.144, s32[16,512]{1,0:T(8,128)S(1)} %eq.147), kind=kOutput, calls=%fused_computation.7.clone.1 | convolution fusion | flops 26218496 | bytes 114692 | tf_op jit(solution)/shard_map/while/body/eval_jaxpr/gps,cgp->csg/dot_general | solution.py:38
  44.1 7.4 %all-to-all-start = ((f32[8,9,32,128]{3,2,1,0:T(8,128)}), f32[8,9,32,128]{3,2,1,0:T(8,128)S(1)}, u32[]{:S(2)}, u32[]{:S(2)}) async-start(f32[8,9,32,128]{3,2,1,0:T(8,128)} %fusion.46), calls=%async_computation | async-start | bytes 2359296 | tf_op jit(solution)/shard_map/all_to_all | solution.py:12
  52.9 27.2 %all-to-all-done = f32[8,9,32,128]{3,2,1,0:T(8,128)S(1)} async-done(((f32[8,9,32,128]{3,2,1,0:T(8,128)}), f32[8,9,32,128]{3,2,1,0:T(8,128)S(1)}, u32[]{:S(2)}, u32[]{:S(2)}) %all-to-all-start) | async-done | bytes 1179680 | tf_op jit(solution)/shard_map/all_to_all | solution.py:12
  93.2 3.6 %all-to-all-start.1 = ((f32[32,8,128]{2,0,1:T(8,128)}), f32[32,8,128]{2,0,1:T(8,128)S(1)}, u32[]{:S(2)}, u32[]{:S(2)}) async-start(f32[32,8,128]{2,0,1:T(8,128)} %copy.45), calls=%async_computation.1 | async-start | bytes 262144 | tf_op jit(solution)/shard_map/all_to_all | solution.py:126
  100.5 3.7 %all-to-all-done.1 = f32[32,8,128]{2,0,1:T(8,128)S(1)} async-done(((f32[32,8,128]{2,0,1:T(8,128)}), f32[32,8,128]{2,0,1:T(8,128)S(1)}, u32[]{:S(2)}, u32[]{:S(2)}) %all-to-all-start.1) | async-done | bytes 131104 | tf_op jit(solution)/shard_map/all_to_all | solution.py:126
  104.7 86.0 %while.31 = (s32[]{:T(128)}, f32[4,65536]{1,0:T(4,128)S(1)}, f32[]{:T(128)}, f32[4,65536]{1,0:T(4,128)}, f32[2,128,128]{1,2,0:T(8,128)S(1)}, /*index=5*/s32[6553...) while((s32[]{:T(128)}, f32[4,65536]{1,0:T(4,128)S(1)}, ...), condition=%wide.region_5.6_spmd.clone, body=%wide.region_4.5_spmd.clone.sunk | while | flops 26509320 | bytes 1458525 | solution.py:139
  105.5 2.9 %fusion.177 = f32[2,16,512]{2,0,1:T(2,128)S(1)} fusion(s32[16,512]{1,0:T(8,128)S(1)} %eq.150, f32[2,128,16]{1,2,0:T(8,128)S(1)} %constant_dynamic-slice_fusion.5), kind=kOutput, calls=%fused_computation.12.clone.1 | convolution fusion | flops 26214400 | bytes 114688 | tf_op jit(solution)/shard_map/while/body/eval_jaxpr/gps,csg->cgp/dot_general | solution.py:38
  108.5 1.9 %fusion.179 = (f32[1,8192]{1,0:T(1,128)S(1)}, f32[1,8192]{1,0:T(1,128)S(1)}, f32[1,8192]{1,0:T(1,128)S(1)}) fusion(f32[]{:T(128)} %get-tuple-element.591, f32[4,65536]{1,0:T(4,128)} %get-tuple-element.588, s32[]{:T(128)S(6)} %select_n.186, f32[]{:T(128)} %get-tuple-element.587, f32[1,8192]{1,0:T(1,128)S(1)} %bitcast.143, s32[]{:T(128)S(6)} %add.419), kind=kLoop, calls=%fused_computation.194.clone.1 | loop fusion | flops 49152 | bytes 196624 | tf_op jit(solution)/shard_map/while/body/eval_jaxpr/cos | solution.py:23
  110.4 3.0 %multiply_add_fusion.11 = (f32[1,8192]{1,0:T(1,128)S(1)}, f32[1,8192]{1,0:T(1,128)S(1)}, f32[1,8192]{1,0:T(1,128)S(1)}, f32[1,8192]{1,0:T(1,128)S(1)}, f32[1,8192]{1,0:T(1,128)S(1)}) fusion(f32[1,8192]{1,0:T(1,128)S(1)} %get-tuple-element.508, f32[1,8192]{1,0:T(1,128)S(1)} %get-tuple-element.509, f32[4,65536]{1,0:T(4,128)} %get-tuple-element.588, ...), kind=kLoop, calls=%fused_computation.20.clone.1 | loop fusion | flops 98304 | bytes 393236 | tf_op jit(solution)/shard_map/while/body/eval_jaxpr/add | solution.py:25
  116.2 2.9 %fusion.177 = f32[2,16,512]{2,0,1:T(2,128)S(1)} fusion(s32[16,512]{1,0:T(8,128)S(1)} %eq.150, f32[2,128,16]{1,2,0:T(8,128)S(1)} %constant_dynamic-slice_fusion.5), kind=kOutput, calls=%fused_computation.12.clone.1 | convolution fusion | flops 26214400 | bytes 114688 | tf_op jit(solution)/shard_map/while/body/eval_jaxpr/gps,csg->cgp/dot_general | solution.py:38
  119.2 1.9 %fusion.179 = (f32[1,8192]{1,0:T(1,128)S(1)}, f32[1,8192]{1,0:T(1,128)S(1)}, f32[1,8192]{1,0:T(1,128)S(1)}) fusion(f32[]{:T(128)} %get-tuple-element.591, f32[4,65536]{1,0:T(4,128)} %get-tuple-element.588, s32[]{:T(128)S(6)} %select_n.186, f32[]{:T(128)} %get-tuple-element.587, f32[1,8192]{1,0:T(1,128)S(1)} %bitcast.143, s32[]{:T(128)S(6)} %add.419), kind=kLoop, calls=%fused_computation.194.clone.1 | loop fusion | flops 49152 | bytes 196624 | tf_op jit(solution)/shard_map/while/body/eval_jaxpr/cos | solution.py:23
  121.2 3.0 %multiply_add_fusion.11 = (f32[1,8192]{1,0:T(1,128)S(1)}, f32[1,8192]{1,0:T(1,128)S(1)}, f32[1,8192]{1,0:T(1,128)S(1)}, f32[1,8192]{1,0:T(1,128)S(1)}, f32[1,8192]{1,0:T(1,128)S(1)}) fusion(f32[1,8192]{1,0:T(1,128)S(1)} %get-tuple-element.508, f32[1,8192]{1,0:T(1,128)S(1)} %get-tuple-element.509, f32[4,65536]{1,0:T(4,128)} %get-tuple-element.588, ...), kind=kLoop, calls=%fused_computation.20.clone.1 | loop fusion | flops 98304 | bytes 393236 | tf_op jit(solution)/shard_map/while/body/eval_jaxpr/add | solution.py:25
  127.0 2.9 %fusion.177 = f32[2,16,512]{2,0,1:T(2,128)S(1)} fusion(s32[16,512]{1,0:T(8,128)S(1)} %eq.150, f32[2,128,16]{1,2,0:T(8,128)S(1)} %constant_dynamic-slice_fusion.5), kind=kOutput, calls=%fused_computation.12.clone.1 | convolution fusion | flops 26214400 | bytes 114688 | tf_op jit(solution)/shard_map/while/body/eval_jaxpr/gps,csg->cgp/dot_general | solution.py:38
  131.9 3.0 %multiply_add_fusion.11 = (f32[1,8192]{1,0:T(1,128)S(1)}, f32[1,8192]{1,0:T(1,128)S(1)}, f32[1,8192]{1,0:T(1,128)S(1)}, f32[1,8192]{1,0:T(1,128)S(1)}, f32[1,8192]{1,0:T(1,128)S(1)}) fusion(f32[1,8192]{1,0:T(1,128)S(1)} %get-tuple-element.508, f32[1,8192]{1,0:T(1,128)S(1)} %get-tuple-element.509, f32[4,65536]{1,0:T(4,128)} %get-tuple-element.588, ...), kind=kLoop, calls=%fused_computation.20.clone.1 | loop fusion | flops 98304 | bytes 393236 | tf_op jit(solution)/shard_map/while/body/eval_jaxpr/add | solution.py:25
  137.7 2.9 %fusion.177 = f32[2,16,512]{2,0,1:T(2,128)S(1)} fusion(s32[16,512]{1,0:T(8,128)S(1)} %eq.150, f32[2,128,16]{1,2,0:T(8,128)S(1)} %constant_dynamic-slice_fusion.5), kind=kOutput, calls=%fused_computation.12.clone.1 | convolution fusion | flops 26214400 | bytes 114688 | tf_op jit(solution)/shard_map/while/body/eval_jaxpr/gps,csg->cgp/dot_general | solution.py:38
  142.7 3.0 %multiply_add_fusion.11 = (f32[1,8192]{1,0:T(1,128)S(1)}, f32[1,8192]{1,0:T(1,128)S(1)}, f32[1,8192]{1,0:T(1,128)S(1)}, f32[1,8192]{1,0:T(1,128)S(1)}, f32[1,8192]{1,0:T(1,128)S(1)}) fusion(f32[1,8192]{1,0:T(1,128)S(1)} %get-tuple-element.508, f32[1,8192]{1,0:T(1,128)S(1)} %get-tuple-element.509, f32[4,65536]{1,0:T(4,128)} %get-tuple-element.588, ...), kind=kLoop, calls=%fused_computation.20.clone.1 | loop fusion | flops 98304 | bytes 393236 | tf_op jit(solution)/shard_map/while/body/eval_jaxpr/add | solution.py:25
  148.5 2.9 %fusion.177 = f32[2,16,512]{2,0,1:T(2,128)S(1)} fusion(s32[16,512]{1,0:T(8,128)S(1)} %eq.150, f32[2,128,16]{1,2,0:T(8,128)S(1)} %constant_dynamic-slice_fusion.5), kind=kOutput, calls=%fused_computation.12.clone.1 | convolution fusion | flops 26214400 | bytes 114688 | tf_op jit(solution)/shard_map/while/body/eval_jaxpr/gps,csg->cgp/dot_general | solution.py:38
  153.4 3.0 %multiply_add_fusion.11 = (f32[1,8192]{1,0:T(1,128)S(1)}, f32[1,8192]{1,0:T(1,128)S(1)}, f32[1,8192]{1,0:T(1,128)S(1)}, f32[1,8192]{1,0:T(1,128)S(1)}, f32[1,8192]{1,0:T(1,128)S(1)}) fusion(f32[1,8192]{1,0:T(1,128)S(1)} %get-tuple-element.508, f32[1,8192]{1,0:T(1,128)S(1)} %get-tuple-element.509, f32[4,65536]{1,0:T(4,128)} %get-tuple-element.588, ...), kind=kLoop, calls=%fused_computation.20.clone.1 | loop fusion | flops 98304 | bytes 393236 | tf_op jit(solution)/shard_map/while/body/eval_jaxpr/add | solution.py:25
  159.2 2.9 %fusion.177 = f32[2,16,512]{2,0,1:T(2,128)S(1)} fusion(s32[16,512]{1,0:T(8,128)S(1)} %eq.150, f32[2,128,16]{1,2,0:T(8,128)S(1)} %constant_dynamic-slice_fusion.5), kind=kOutput, calls=%fused_computation.12.clone.1 | convolution fusion | flops 26214400 | bytes 114688 | tf_op jit(solution)/shard_map/while/body/eval_jaxpr/gps,csg->cgp/dot_general | solution.py:38
  164.2 3.0 %multiply_add_fusion.11 = (f32[1,8192]{1,0:T(1,128)S(1)}, f32[1,8192]{1,0:T(1,128)S(1)}, f32[1,8192]{1,0:T(1,128)S(1)}, f32[1,8192]{1,0:T(1,128)S(1)}, f32[1,8192]{1,0:T(1,128)S(1)}) fusion(f32[1,8192]{1,0:T(1,128)S(1)} %get-tuple-element.508, f32[1,8192]{1,0:T(1,128)S(1)} %get-tuple-element.509, f32[4,65536]{1,0:T(4,128)} %get-tuple-element.588, ...), kind=kLoop, calls=%fused_computation.20.clone.1 | loop fusion | flops 98304 | bytes 393236 | tf_op jit(solution)/shard_map/while/body/eval_jaxpr/add | solution.py:25
  170.0 2.9 %fusion.177 = f32[2,16,512]{2,0,1:T(2,128)S(1)} fusion(s32[16,512]{1,0:T(8,128)S(1)} %eq.150, f32[2,128,16]{1,2,0:T(8,128)S(1)} %constant_dynamic-slice_fusion.5), kind=kOutput, calls=%fused_computation.12.clone.1 | convolution fusion | flops 26214400 | bytes 114688 | tf_op jit(solution)/shard_map/while/body/eval_jaxpr/gps,csg->cgp/dot_general | solution.py:38
  174.9 3.0 %multiply_add_fusion.11 = (f32[1,8192]{1,0:T(1,128)S(1)}, f32[1,8192]{1,0:T(1,128)S(1)}, f32[1,8192]{1,0:T(1,128)S(1)}, f32[1,8192]{1,0:T(1,128)S(1)}, f32[1,8192]{1,0:T(1,128)S(1)}) fusion(f32[1,8192]{1,0:T(1,128)S(1)} %get-tuple-element.508, f32[1,8192]{1,0:T(1,128)S(1)} %get-tuple-element.509, f32[4,65536]{1,0:T(4,128)} %get-tuple-element.588, ...), kind=kLoop, calls=%fused_computation.20.clone.1 | loop fusion | flops 98304 | bytes 393236 | tf_op jit(solution)/shard_map/while/body/eval_jaxpr/add | solution.py:25
  180.7 2.9 %fusion.177 = f32[2,16,512]{2,0,1:T(2,128)S(1)} fusion(s32[16,512]{1,0:T(8,128)S(1)} %eq.150, f32[2,128,16]{1,2,0:T(8,128)S(1)} %constant_dynamic-slice_fusion.5), kind=kOutput, calls=%fused_computation.12.clone.1 | convolution fusion | flops 26214400 | bytes 114688 | tf_op jit(solution)/shard_map/while/body/eval_jaxpr/gps,csg->cgp/dot_general | solution.py:38
  185.7 3.0 %multiply_add_fusion.11 = (f32[1,8192]{1,0:T(1,128)S(1)}, f32[1,8192]{1,0:T(1,128)S(1)}, f32[1,8192]{1,0:T(1,128)S(1)}, f32[1,8192]{1,0:T(1,128)S(1)}, f32[1,8192]{1,0:T(1,128)S(1)}) fusion(f32[1,8192]{1,0:T(1,128)S(1)} %get-tuple-element.508, f32[1,8192]{1,0:T(1,128)S(1)} %get-tuple-element.509, f32[4,65536]{1,0:T(4,128)} %get-tuple-element.588, ...), kind=kLoop, calls=%fused_computation.20.clone.1 | loop fusion | flops 98304 | bytes 393236 | tf_op jit(solution)/shard_map/while/body/eval_jaxpr/add | solution.py:25
  (133 shorter events, 75.0 us)
Async XLA Ops:
  0.6 103.5 %copy-start = (f32[128,128]{1,0:T(8,128)S(1)}, f32[128,128]{1,0:T(8,128)}, u32[]{:S(2)}) copy-start(f32[128,128]{1,0:T(8,128)} %param.15) | copy-start | bytes 196612
  0.7 38.1 %copy-start.1 = (f32[8,2,128,128]{3,2,1,0:T(8,128)S(1)}, f32[8,2,128,128]{3,2,1,0:T(8,128)}, u32[]{:S(2)}) copy-start(f32[8,2,128,128]{3,2,1,0:T(8,128)} %param.13) | copy-start | bytes 3145732
  38.7 4.7 %copy-start.2 = (f32[2,128,128]{2,1,0:T(8,128)}, f32[2,128,128]{2,1,0:T(8,128)S(1)}, u32[]{:S(2)}) copy-start(f32[2,128,128]{2,1,0:T(8,128)S(1)} %copy.40) | copy-start | bytes 393220
  44.1 7.4 %copy-start.4 = (f32[9,2,1024]{2,1,0:T(2,128)S(1)}, f32[9,2,1024]{2,1,0:T(2,128)}, u32[]{:S(2)}) copy-start(f32[9,2,1024]{2,1,0:T(2,128)} %param.14) | copy-start | bytes 221188
  44.1 36.0 %all-to-all-start = ((f32[8,9,32,128]{3,2,1,0:T(8,128)}), f32[8,9,32,128]{3,2,1,0:T(8,128)S(1)}, u32[]{:S(2)}, u32[]{:S(2)}) async-start(f32[8,9,32,128]{3,2,1,0:T(8,128)} %fusion.46), calls=%async_computation | async-start | bytes 2359296 | tf_op jit(solution)/shard_map/all_to_all | solution.py:12
  90.6 6.2 %copy-start.5 = (f32[2]{0:T(128)S(1)}, f32[2]{0:T(128)}, u32[]{:S(2)}) copy-start(f32[2]{0:T(128)} %param.16) | copy-start | bytes 28
  90.6 8.0 %copy-start.6 = (f32[2]{0:T(128)S(1)}, f32[2]{0:T(128)}, u32[]{:S(2)}) copy-start(f32[2]{0:T(128)} %param.17) | copy-start | bytes 28
  93.2 11.0 %all-to-all-start.1 = ((f32[32,8,128]{2,0,1:T(8,128)}), f32[32,8,128]{2,0,1:T(8,128)S(1)}, u32[]{:S(2)}, u32[]{:S(2)}) async-start(f32[32,8,128]{2,0,1:T(8,128)} %copy.45), calls=%async_computation.1 | async-start | bytes 262144 | tf_op jit(solution)/shard_map/all_to_all | solution.py:126
  190.7 1.0 copy-start.3
